TPU v7x, 32 devices: a whole 2x2x4 slice. The times are simulated.
32 devices in a mesh: beam: 2 (over x), tm: 16 (over z, y, core).
Axes of the slice: x: 2, y: 2, z: 4, core: 2. Of those that a mesh axis runs over, the one named last changes fastest.
Arguments:
- voltage: bfloat16 [2, 2, 2097152], P(None, None, ('beam', 'tm')), parts along dimension 2, may hold values from -11 to 11
- delays: int32 [64, 2048], replicated, may hold values from 0 to 96, as said below
- chan_mask: int32 [4096], P('beam'), parts along dimension 0, may hold values 0 or 1
Outputs:
- zscore: float32 [64, 1024], P(None, ('beam', 'tm')), parts along dimension 1
- trial_stats: float32 [3, 128], P(None, 'beam'), parts along dimension 1
There are 2 independent parts, one for each index of `beam`. A program takes and returns all parts, laid end to end along the dimension named above; an argument that names none is the same for every part. Nothing has to cross between parts.
Inputs may be any that keep to these rules, and one draw needn't show every extreme that they name: For each trial the delays never rise from one channel to the next; the last channel's delays are 0, and the first channel's delay of some trial is 96.
All inputs are finite; a program needn't handle non-finite values.
Results may differ from a plain program's by a relative error of at most 0.002.
Values may be sent and summed in bfloat16 or wider, within the bound.
A program may use at most 64 MiB of HBM per device.

v0:
```python
import math

import jax
import jax.numpy as jnp
from jax import lax
from jax.sharding import PartitionSpec as P

NCHAN = 2048
TAPS = 16
DSPAN = 3


highest = lax.Precision.HIGHEST
shift_group = 8


def passed_along(value, axis, steps):
    count = lax.axis_size(axis)
    first, last = (max(0, -steps), min(count, count - steps))
    return lax.ppermute(value, axis, [(source, source + steps) for source in range(first, last)])


def prototype(tap_count, chan_count):
    length = tap_count * chan_count
    position = jnp.arange(length, dtype=jnp.float32)
    centred = (position - (length - 1) / 2.0) / chan_count
    window = 0.54 - 0.46 * jnp.cos(2.0 * jnp.pi * position / (length - 1))
    shaped = jnp.sinc(centred) * window
    shaped = shaped * jnp.sqrt(chan_count / jnp.sum(shaped * shaped))
    return shaped.reshape(tap_count, chan_count)


def phase_table(row_count, col_count, period):
    product = (
        jnp.arange(row_count, dtype=jnp.int32)[:, None]
        * jnp.arange(col_count, dtype=jnp.int32)[None, :]
        % period
    )
    angles = product.astype(jnp.float32) * (-2.0 * jnp.pi / period)
    return (jnp.cos(angles), jnp.sin(angles))


def spectral_power(weighted, chan_count):
    frame_count = weighted.shape[2]
    low_count = chan_count // 128
    split_up = weighted.reshape(2, 2, frame_count, low_count, 128)
    real_part = split_up[:, 0]
    imag_part = split_up[:, 1]
    cos_first, sin_first = phase_table(low_count, low_count, low_count)
    section_real = jnp.einsum(
        "pfmn,mk->pfkn", real_part, cos_first, precision=highest
    ) - jnp.einsum("pfmn,mk->pfkn", imag_part, sin_first, precision=highest)
    section_imag = jnp.einsum(
        "pfmn,mk->pfkn", real_part, sin_first, precision=highest
    ) + jnp.einsum("pfmn,mk->pfkn", imag_part, cos_first, precision=highest)
    cos_twist, sin_twist = phase_table(low_count, 128, chan_count)
    twist_real = section_real * cos_twist - section_imag * sin_twist
    twist_imag = section_real * sin_twist + section_imag * cos_twist
    cos_second, sin_second = phase_table(128, 128, 128)
    scale_factor = 1.0 / math.sqrt(chan_count)
    cos_second = cos_second * scale_factor
    sin_second = sin_second * scale_factor
    final_real = jnp.einsum(
        "pfkn,nj->pfkj", twist_real, cos_second, precision=highest
    ) - jnp.einsum("pfkn,nj->pfkj", twist_imag, sin_second, precision=highest)
    final_imag = jnp.einsum(
        "pfkn,nj->pfkj", twist_real, sin_second, precision=highest
    ) + jnp.einsum("pfkn,nj->pfkj", twist_imag, cos_second, precision=highest)
    energy = jnp.sum(final_real * final_real + final_imag * final_imag, axis=0)
    return jnp.transpose(energy, (2, 1, 0)).reshape(chan_count, frame_count).astype(jnp.bfloat16)


def dedisperse(padded, delays, out_width, max_delay):
    chan_count = padded.shape[0]
    group_count = (max_delay + shift_group) // shift_group
    needed = out_width + group_count * shift_group
    padded = jnp.concatenate(
        [padded, jnp.zeros((chan_count, needed - padded.shape[1]), padded.dtype)], axis=1
    )
    within = jnp.arange(shift_group, dtype=jnp.int32)

    def add_group(group_index, running):
        base = (group_index * shift_group).astype(jnp.int32)
        window = lax.dynamic_slice_in_dim(padded, base, out_width + shift_group - 1, 1)
        stacked = jnp.stack(
            [window[:, offset : offset + out_width] for offset in range(shift_group)]
        )
        targets = base + within
        selector = (delays[:, None, :] == targets[None, :, None]).astype(jnp.bfloat16)
        return running + jnp.einsum(
            "dsk,skt->dt", selector, stacked, preferred_element_type=jnp.float32
        )

    zero_sums = jnp.zeros((delays.shape[0], out_width), jnp.float32)
    return lax.fori_loop(0, group_count, add_group, zero_sums)


def per_device(voltage, delays, chan_mask):
    frame_count = voltage.shape[2] // NCHAN
    framed = voltage.reshape(2, 2, frame_count, NCHAN)
    history = passed_along(framed[:, :, frame_count - (TAPS - 1) :], "tm", 1)
    extended = jnp.concatenate([history, framed], axis=2)
    coeffs = prototype(TAPS, NCHAN)
    weighted = jnp.zeros((2, 2, frame_count, NCHAN), jnp.float32)
    for tap_index in range(TAPS):
        weighted = weighted + coeffs[tap_index] * extended[
            :, :, tap_index : tap_index + frame_count
        ].astype(jnp.float32)
    detected = spectral_power(weighted, NCHAN)
    masked = detected * chan_mask.astype(jnp.bfloat16)[:, None]
    max_delay = DSPAN * frame_count
    gathered = masked
    held_shards = 1
    while held_shards < DSPAN + 1:
        fetched = passed_along(gathered, "tm", -held_shards)
        gathered = jnp.concatenate([gathered, fetched], axis=1)
        held_shards = held_shards * 2
    series = dedisperse(gathered, delays, frame_count, max_delay)
    local_frames = series.shape[1]
    total_frames = local_frames * lax.axis_size("tm")
    totals = lax.psum(jnp.sum(series, axis=1), "tm")
    peak_value = lax.pmax(jnp.max(series, axis=1), "tm")
    average = totals / total_frames
    centred = series - average[:, None]
    variance = lax.psum(jnp.sum(centred * centred, axis=1), "tm") / total_frames
    deviation = jnp.sqrt(variance + 1e-05)
    zscore = centred / deviation[:, None]
    live_count = jnp.maximum(jnp.sum(chan_mask).astype(jnp.float32), 1.0)
    trial_stats = jnp.stack(
        [average / live_count, deviation / live_count, (peak_value - average) / deviation]
    )
    return (zscore, trial_stats)


def solution(mesh):
    in_specs = (P(None, None, ("beam", "tm")), P(), P("beam"))
    out_specs = (P(None, ("beam", "tm")), P(None, "beam"))
    return jax.shard_map(
        per_device, mesh=mesh, in_specs=in_specs, out_specs=out_specs, check_vma=False
    )
```

profile of v0, /device:TPU:0, one launch (start us, length us, event | category | flops | bytes accessed | tf_op | source)
XLA Modules:
  0.0 158.4 jit_solution(6258443623836400769)
XLA Ops:
  0.6 1.4 reshape.106
  2.0 0.0 copy-start
  2.1 0.1 slice.217
  2.2 2.4 %collective-permute-start = (bf16[2,2,15,2048]{3,2,0,1:T(8,128)(2,1)S(1)}, bf16[2,2,15,2048]{3,2,0,1:T(8,128)(2,1)S(1)}, u32[]{:S(2)}, u32[]{:S(2)}) collective-permute-start(bf16[2,2,15,2048]{3,2,0,1:T(8,128)(2,1)S(1)} %slice.217), channel_id=1, source_target_pairs={{0,1},{1,2},{2,3},{3,4},{4,5},{5,6},{6,7},{7,8},{8,9},{9,10},{10,1... | collective-permute-start | bytes 737288 | tf_op jit(solution)/shard_map/ppermute | solution.py:20
  4.6 1.2 multiply_reduce_fusion
  6.6 0.6 broadcast_multiply_fusion
  7.2 0.0 copy-done
  7.2 0.6 fusion.155
  7.8 0.1 fusion.108
  7.9 0.0 collective-permute-done
  7.9 2.6 %multiply_add_fusion = f32[2,2,32,2048]{3,2,0,1:T(8,128)S(1)} fusion(bf16[2,2,32,2048]{3,2,0,1:T(8,128)(2,1)S(1)} %copy.12, bf16[2,2,15,2048]{3,2,0,1:T(8,128)(2,1)S(1)} %collective-permute-done, f32[2048]{0:T(1024)S(1)} %get-tuple-element.133, f32[2048]{0:T(1024)S(1)} %get-tuple-element.134, f32[2048]{0:T(1024)S(1)} %get-tuple-element.135, ...), kind=kLoop, calls=%fused_computation.61 | loop fusion | flops 24117248 | bytes 1949696 | tf_op jit(solution)/shard_map/add | solution.py:106
  10.6 0.2 copy.21
  10.8 0.6 fusion.45
  11.4 0.6 fusion.44
  12.0 0.6 convolution_subtract_fusion.1
  12.6 0.6 convolution_add_fusion.1
  13.2 0.8 fusion.40
  14.1 0.8 fusion.42
  14.9 0.8 fusion.22
  15.7 0.8 fusion.23
  16.6 0.5 copy.15
  17.1 0.3 bitcast_multiply_fusion
  17.4 1.3 collective-permute-start.1
  18.7 4.6 %collective-permute-done.1 = bf16[2048,32]{1,0:T(8,128)(2,1)S(1)} collective-permute-done((bf16[2048,32]{1,0:T(8,128)(2,1)S(1)}, bf16[2048,32]{1,0:T(8,128)(2,1)S(1)}, u32[]{:S(2)}, u32[]{:S(2)}) %collective-permute-start.1) | collective-permute-done | bytes 131104 | tf_op jit(solution)/shard_map/ppermute | solution.py:20
  23.3 0.3 pad_maximum_fusion.1
  23.6 1.5 collective-permute-start.2
  25.8 18.1 %collective-permute-done.2 = bf16[2048,64]{1,0:T(8,128)(2,1)S(1)} collective-permute-done((bf16[2048,64]{1,0:T(8,128)(2,1)S(1)}, bf16[2048,64]{1,0:T(8,128)(2,1)S(1)}, u32[]{:S(2)}, u32[]{:S(2)}) %collective-permute-start.2) | collective-permute-done | bytes 262176 | tf_op jit(solution)/shard_map/ppermute | solution.py:20
  43.9 0.9 maximum_maximum_fusion
  44.8 0.0 copy-start.1
  44.8 0.4 copy.16
  45.3 0.6 copy-done.1
  45.8 17.2 %while.14 = (s32[]{:T(128)}, f32[64,32]{0,1:T(8,128)S(1)}, s32[64,2048]{1,0:T(8,128)S(1)}, bf16[2048,136]{0,1:T(8,128)(2,1)S(1)}, s32[]{:T(128)}, /*index=5*/s32...) while((s32[]{:T(128)}, f32[64,32]{0,1:T(8,128)S(1)}, ...), condition=%wide.region_3.4_spmd.clone, body=%wide.region_2.3_spmd.clone.sunk | while | flops 68161560 | bytes 3686781 | solution.py:95
  46.2 0.9 fusion.178
  47.6 0.9 fusion.178
  48.9 0.9 fusion.178
  50.2 0.9 fusion.178
  51.6 0.9 fusion.178
  52.9 0.9 fusion.178
  54.2 0.9 fusion.178
  55.5 0.9 fusion.178
  56.9 0.9 fusion.178
  58.2 0.9 fusion.178
  59.5 0.9 fusion.178
  60.9 0.9 fusion.178
  62.2 0.9 fusion.178
  63.1 35.0 %psum.14 = f32[64]{0:T(128)S(1)} all-reduce(f32[64]{0:T(128)S(1)} %get-tuple-element.123), channel_id=1, replica_groups=mesh['beam'=2,'tm'=16] {'tm'}, use_global_device_ids=true, to_apply=%region_5.6 | all-reduce | flops 64 | bytes 512 | tf_op jit(solution)/shard_map/psum | solution.py:121
  98.2 29.5 %psum.15 = f32[64]{0:T(128)S(1)} all-reduce(f32[64]{0:T(128)S(1)} %multiply_reduce_fusion.1), channel_id=1, replica_groups=mesh['beam'=2,'tm'=16] {'tm'}, use_global_device_ids=true, to_apply=%region_7.8 | all-reduce | flops 64 | bytes 512 | tf_op jit(solution)/shard_map/psum | solution.py:125
  127.7 29.5 %pmax.7 = f32[64]{0:T(128)S(1)} all-reduce(f32[64]{0:T(128)S(1)} %get-tuple-element.122), channel_id=1, replica_groups=mesh['beam'=2,'tm'=16] {'tm'}, use_global_device_ids=true, to_apply=%region_10.11 | all-reduce | flops 64 | bytes 512 | tf_op jit(solution)/shard_map/pmax | solution.py:122
  157.2 0.6 subtract_divide_fusion
  157.8 0.6 pad_maximum_fusion.2
  (126 shorter events, 4.2 us)
Async XLA Ops:
  2.0 5.2 %copy-start = (s32[2048]{0:T(1024)S(1)}, s32[2048]{0:T(1024)}, u32[]{:S(2)}) copy-start(s32[2048]{0:T(1024)} %param.7) | copy-start | bytes 24580
  2.2 5.8 %collective-permute-start = (bf16[2,2,15,2048]{3,2,0,1:T(8,128)(2,1)S(1)}, bf16[2,2,15,2048]{3,2,0,1:T(8,128)(2,1)S(1)}, u32[]{:S(2)}, u32[]{:S(2)}) collective-permute-start(bf16[2,2,15,2048]{3,2,0,1:T(8,128)(2,1)S(1)} %slice.217), channel_id=1, source_target_pairs={{0,1},{1,2},{2,3},{3,4},{4,5},{5,6},{6,7},{7,8},{8,9},{9,10},{10,1... | collective-permute-start | bytes 737288 | tf_op jit(solution)/shard_map/ppermute | solution.py:20
  17.4 5.9 %collective-permute-start.1 = (bf16[2048,32]{1,0:T(8,128)(2,1)S(1)}, bf16[2048,32]{1,0:T(8,128)(2,1)S(1)}, u32[]{:S(2)}, u32[]{:S(2)}) collective-permute-start(bf16[2048,32]{1,0:T(8,128)(2,1)S(1)} %bitcast_multiply_fusion), channel_id=1, source_target_pairs={{1,0},{2,1},{3,2},{4,3},{5,4},{6,5},{7,6},{8,7},{9,8},{10,9},{11,1... | collective-permute-start | bytes 393224 | tf_op jit(solution)/shard_map/ppermute | solution.py:20
  23.6 20.3 %collective-permute-start.2 = (bf16[2048,64]{1,0:T(8,128)(2,1)S(1)}, bf16[2048,64]{1,0:T(8,128)(2,1)S(1)}, u32[]{:S(2)}, u32[]{:S(2)}) collective-permute-start(bf16[2048,64]{1,0:T(8,128)(2,1)S(1)} %pad_maximum_fusion.1), channel_id=1, source_target_pairs={{2,0},{3,1},{4,2},{5,3},{6,4},{7,5},{8,6},{9,7},{10,8},{11,9},{12,... | collective-permute-start | bytes 786440 | tf_op jit(solution)/shard_map/ppermute | solution.py:20
  44.8 1.0 copy-start.1
where the time goes:
time: 159 us; the launch traced here: 158 us
  blocking collectives  94 us (59%)
  waiting for transfers between devices  22.7 us (14%)
  matrix products  17.3 us (11%)
  other arithmetic  8.09 us (5%)
  local copies, waits for them, and re-layouts  7.21 us (5%)
  starting transfers between devices  5.18 us (3%)
  between operations  2.24 us (1%)
  loops' own time  1.66 us (1%)
    psum x1, blocking collectives, per_device(): totals = lax.psum(jnp.sum(series, axis=1), 'tm')  35 us
    psum x1, blocking collectives, per_device(): variance = lax.psum(jnp.sum(centred * centred, axis=1), 'tm') / total_frames  29.5 us
    pmax x1, blocking collectives, per_device(): peak_value = lax.pmax(jnp.max(series, axis=1), 'tm')  29.5 us
    ppermute x3, waiting for transfers between devices, passed_along(): lax.ppermute(value, axis, [(source, source + steps) for source in range(f...  22.7 us
    dot_general x13, matrix products, add_group(): jnp.einsum('dsk,skt->dt', selector, stacked, preferred_element_type=jnp.f...  11.5 us
    ppermute x3, starting transfers between devices, passed_along(): lax.ppermute(value, axis, [(source, source + steps) for source in range(f...  5.18 us
    while x91, local copies, waits for them, and re-layouts  3.45 us
  transfers between devices with their start and end apart: 3, of which 2 were waited for; matrix products, arithmetic and copies ran while one was open for 2% of the time, Pallas kernels for 0%

commit v1 on v0

v1 whole, which is shorter than its diff:
```python
import functools
import math

import jax
import jax.numpy as jnp
import numpy as np
from jax import lax
from jax.experimental import pallas as pl
from jax.experimental.pallas import tpu as pltpu
from jax.sharding import PartitionSpec as P

NCHAN = 2048
TAPS = 16
DSPAN = 3
LANES = 128
RADIX = NCHAN // LANES
BLOCK = 256
STEP = 4
MESH = pl.DeviceIdType.MESH


def prototype():
    length = TAPS * NCHAN
    position = np.arange(length, dtype=np.float64)
    window = 0.54 - 0.46 * np.cos(2.0 * np.pi * position / (length - 1))
    shaped = np.sinc((position - (length - 1) / 2.0) / NCHAN) * window
    shaped = shaped * np.sqrt(NCHAN / np.sum(shaped * shaped))
    taps = shaped.reshape(TAPS, RADIX, 1, LANES)
    taps = np.broadcast_to(taps, (TAPS, RADIX, 2, LANES))
    return taps.reshape(TAPS, 2 * RADIX, LANES).astype(np.float32)


def twiddles():
    angle = -2.0 * np.pi * np.outer(np.arange(RADIX), np.arange(LANES)) / NCHAN
    return np.stack([np.cos(angle), np.sin(angle)]).astype(np.float32)


def transform_table():
    angle = -2.0 * np.pi * (np.outer(np.arange(LANES), np.arange(LANES)) % LANES) / LANES
    scale = 1.0 / math.sqrt(NCHAN)
    cos, sin = np.cos(angle) * scale, np.sin(angle) * scale
    full = np.block([[cos, sin], [-sin, cos]]).astype(np.float32)
    high = full.astype(jnp.bfloat16)
    low = (full - high.astype(np.float32)).astype(jnp.bfloat16)
    return np.stack([high, low])


def butterflies(items):
    count = len(items)
    if count == 1:
        return items
    even = butterflies(items[0::2])
    odd = butterflies(items[1::2])
    half = count // 2
    out = [None] * count
    for k in range(half):
        re, im = odd[k]
        if k == 0:
            tr, ti = re, im
        elif 4 * k == count:
            tr, ti = im, -re
        elif 8 * k == count:
            r = math.sqrt(0.5)
            tr, ti = (re + im) * r, (im - re) * r
        elif 8 * k == 3 * count:
            r = math.sqrt(0.5)
            tr, ti = (im - re) * r, (re + im) * (-r)
        else:
            c, s = math.cos(2 * math.pi * k / count), -math.sin(2 * math.pi * k / count)
            tr, ti = re * c - im * s, re * s + im * c
        er, ei = even[k]
        out[k] = (er + tr, ei + ti)
        out[k + half] = (er - tr, ei - ti)
    return out


def channelize_kernel(frames, volt_ref, halo_ref, taps_ref, twid_ref, table_ref, mask_ref, out_ref,
                      ext, weighted, power):
    past = TAPS - 1
    lines = 2 * RADIX
    for p in range(2):
        ext[p, 0:past] = halo_ref[p].astype(jnp.float32)
        ext[p, past:past + frames] = volt_ref[p].astype(jnp.float32)
    for part in range(lines // 8):
        rows = pl.ds(8 * part, 8)
        taps = [taps_ref[j, rows, :] for j in range(TAPS)]

        def fir(f, carry):
            for p in range(2):
                terms = [taps[j] * ext[p, f + j, rows, :] for j in range(TAPS)]
                while len(terms) > 1:
                    terms = [a + b for a, b in zip(terms[0::2], terms[1::2])]
                start = pl.multiple_of((p * frames + f) * lines, 8) + 8 * part
                weighted[pl.ds(start, 8), :] = terms[0]
            return carry

        lax.fori_loop(0, frames, fir, 0, unroll=4)

    rows_all = 2 * frames
    group = 8
    high_table = table_ref[0]
    low_table = table_ref[1]
    power[...] = jnp.zeros_like(power)
    sections = [[] for _ in range(RADIX)]
    for g in range(rows_all // group):
        items = []
        for m in range(RADIX):
            pair = []
            for c in range(2):
                start = g * group * lines + 2 * m + c
                pair.append(weighted[pl.ds(start, group, stride=lines), :])
            items.append(tuple(pair))
        for k1, (re, im) in enumerate(butterflies(items)):
            if k1:
                c, s = twid_ref[0, k1:k1 + 1, :], twid_ref[1, k1:k1 + 1, :]
                re, im = re * c - im * s, re * s + im * c
            sections[k1].append(jnp.concatenate([re, im], axis=1))
    for k1 in range(RADIX):
        both = jnp.concatenate(sections[k1], axis=0)
        high = both.astype(jnp.bfloat16)
        low = (both - high.astype(jnp.float32)).astype(jnp.bfloat16)
        dot = functools.partial(jnp.dot, preferred_element_type=jnp.float32)
        spec = dot(high, high_table) + (dot(high, low_table) + dot(low, high_table))
        spec = spec * spec
        energy = spec[:, :LANES] + spec[:, LANES:]
        energy = energy[:frames] + energy[frames:]
        kept = energy.astype(jnp.bfloat16).astype(jnp.float32) * mask_ref[k1:k1 + 1, :]
        padded = jnp.concatenate([jnp.zeros((LANES - frames, LANES), jnp.float32), kept], axis=0)
        power[pl.ds(k1, LANES, stride=RADIX), :] = padded.T
    out_ref[...] = power[...].astype(jnp.bfloat16)


def dedisperse_kernel(frames, delay_ref, power_ref, out_ref, acc):
    trials = delay_ref.shape[0]
    reach = LANES - frames
    bits = max(1, reach.bit_length())
    total = jnp.zeros((trials, LANES), jnp.float32)
    for b in range(NCHAN // BLOCK):
        block = delay_ref[:, b * BLOCK:(b + 1) * BLOCK]
        base = block[:, BLOCK - 1:BLOCK]
        relative = block - base
        most = jnp.max(relative[:, 0:1])
        values = power_ref[b * BLOCK:(b + 1) * BLOCK, :]
        acc[...] = jnp.zeros_like(acc)

        def step(i, carry):
            first = i * STEP
            shifted = relative - first
            picks = [jnp.where(shifted == r, 1.0, 0.0).astype(jnp.bfloat16) for r in range(STEP)]
            sums = jnp.dot(jnp.concatenate(picks, axis=0), values, preferred_element_type=jnp.float32)
            run = sums[:trials]
            for r in range(1, STEP):
                run = run + pltpu.roll(sums[r * trials:(r + 1) * trials], LANES - r, 1)
            acc[...] += pltpu.roll(run, lax.rem(2 * LANES - first, LANES), 1)
            return carry

        lax.fori_loop(0, lax.div(most, STEP) + 1, step, 0)
        moved = acc[...]
        for bit in range(bits):
            chosen = ((base >> bit) & 1) == 1
            moved = jnp.where(chosen, pltpu.roll(moved, LANES - (1 << bit), 1), moved)
        total = total + moved
    turned = jnp.concatenate([total, jnp.zeros((LANES - trials, LANES), jnp.float32)], axis=0).T
    half = frames // 2
    for s in range(LANES // frames):
        top = turned[s * frames:s * frames + half]
        low = turned[s * frames + half:(s + 1) * frames]
        out_ref[s * half:(s + 1) * half, :] = top + pltpu.roll(low, trials, 1)


def combine_kernel(count, frames, part_ref, mask_ref, z_ref, stats_ref, landed, mine, gathered, near_send, near_recv,
                   far_send, far_recv):
    me = lax.axis_index("tm")
    half = frames // 2
    trials = LANES // 2
    barrier = pltpu.get_barrier_semaphore()
    for k in range(1, count):
        pl.semaphore_signal(barrier, inc=1, device_id={"tm": lax.rem(me + k, count)}, device_id_type=MESH)
    pl.semaphore_wait(barrier, count - 1)

    def near(k):
        return pltpu.make_async_remote_copy(
            src_ref=part_ref.at[pl.ds((DSPAN - k) * half, half)],
            dst_ref=landed.at[k - 1],
            send_sem=near_send.at[k - 1],
            recv_sem=near_recv.at[k - 1],
            device_id={"tm": me - k},
            device_id_type=MESH,
        )

    for k in range(1, DSPAN + 1):
        @pl.when(me >= k)
        def _():
            near(k).start()

        @pl.when(me < k)
        def _():
            pass

    series = part_ref[DSPAN * half:(DSPAN + 1) * half, :]
    for k in range(1, DSPAN + 1):
        @pl.when(me + k >= count)
        def _():
            landed[k - 1] = jnp.zeros((half, LANES), jnp.float32)

        @pl.when(me + k < count)
        def _():
            near(k).wait_recv()
    for k in range(1, DSPAN + 1):
        series = series + landed[k - 1]

    def fold(value, op):
        return op(value, pltpu.roll(value, trials, 1))

    mean = fold(jnp.sum(series, axis=0, keepdims=True), jnp.add) * (1.0 / frames)
    away = series - mean
    spread = fold(jnp.sum(away * away, axis=0, keepdims=True), jnp.add)
    peak = fold(jnp.max(series, axis=0, keepdims=True), jnp.maximum)
    mine[...] = jnp.concatenate([mean, spread, peak, jnp.zeros((5, LANES), jnp.float32)], axis=0)

    def far(k):
        return pltpu.make_async_remote_copy(
            src_ref=mine,
            dst_ref=gathered.at[k - 1],
            send_sem=far_send.at[k - 1],
            recv_sem=far_recv.at[k - 1],
            device_id={"tm": lax.rem(me + k, count)},
            device_id_type=MESH,
        )

    for k in range(1, count):
        far(k).start()
    live = jnp.maximum(jnp.sum(mask_ref[...].astype(jnp.float32)), 1.0)
    for k in range(1, count):
        far(k).wait_recv()
    everyone = gathered[...]
    average = (mean + jnp.sum(everyone[:, 0:1, :], axis=0)) * (1.0 / count)
    offset = everyone[:, 0:1, :] - average[None]
    squares = spread + jnp.sum(everyone[:, 1:2, :], axis=0)
    between = (mean - average) * (mean - average) + jnp.sum(offset * offset, axis=0)
    variance = (squares + frames * between) * (1.0 / (frames * count))
    top = jnp.maximum(peak, jnp.max(everyone[:, 2:3, :], axis=0))
    deviation = jnp.sqrt(variance + 1e-05)
    z = (series - average) / deviation
    z = jnp.concatenate([z, pltpu.roll(z, trials, 1), jnp.zeros((LANES - frames, LANES), jnp.float32)], axis=0).T
    z_ref[...] = z[:trials, :frames]
    stats_ref[...] = jnp.concatenate(
        [average / live, deviation / live, (top - average) / deviation], axis=0
    )[:, :trials]
    for k in range(1, DSPAN + 1):
        @pl.when(me >= k)
        def _():
            near(k).wait_send()
    for k in range(1, count):
        far(k).wait_send()


def per_device(voltage, delays, chan_mask):
    frames = voltage.shape[2] // NCHAN
    trials = delays.shape[0]
    count = lax.axis_size("tm")
    vmem = pl.BlockSpec(memory_space=pltpu.VMEM)
    lines = 2 * RADIX
    framed = voltage.reshape(2, 2, frames * RADIX, LANES).transpose(0, 2, 1, 3).reshape(2, frames, lines, LANES)
    steps = [(source, source + 1) for source in range(count - 1)]
    halo = lax.ppermute(framed[:, frames - (TAPS - 1):], "tm", steps)
    mask_table = chan_mask.astype(jnp.float32).reshape(LANES, RADIX).T
    power = pl.pallas_call(
        functools.partial(channelize_kernel, frames),
        out_shape=jax.ShapeDtypeStruct((NCHAN, LANES), jnp.bfloat16),
        in_specs=[vmem] * 6,
        out_specs=vmem,
        scratch_shapes=[
            pltpu.VMEM((2, frames + TAPS - 1, lines, LANES), jnp.float32),
            pltpu.VMEM((2 * frames * lines, LANES), jnp.float32),
            pltpu.VMEM((NCHAN, LANES), jnp.float32),
        ],
        name="channelize",
    )(framed, halo, jnp.asarray(prototype()), jnp.asarray(twiddles()), jnp.asarray(transform_table()), mask_table)
    partial = pl.pallas_call(
        functools.partial(dedisperse_kernel, frames),
        out_shape=jax.ShapeDtypeStruct((2 * trials * LANES // LANES // 2, LANES), jnp.float32),
        in_specs=[vmem] * 2,
        out_specs=vmem,
        scratch_shapes=[pltpu.VMEM((trials, LANES), jnp.float32)],
        name="dedisperse",
    )(delays, power)
    zscore, trial_stats = pl.pallas_call(
        functools.partial(combine_kernel, count, frames),
        out_shape=(
            jax.ShapeDtypeStruct((trials, frames), jnp.float32),
            jax.ShapeDtypeStruct((3, trials), jnp.float32),
        ),
        in_specs=[vmem] * 2,
        out_specs=(vmem, vmem),
        scratch_shapes=[
            pltpu.VMEM((DSPAN, frames // 2, LANES), jnp.float32),
            pltpu.VMEM((8, LANES), jnp.float32),
            pltpu.VMEM((count - 1, 8, LANES), jnp.float32),
            pltpu.SemaphoreType.DMA((DSPAN,)),
            pltpu.SemaphoreType.DMA((DSPAN,)),
            pltpu.SemaphoreType.DMA((count - 1,)),
            pltpu.SemaphoreType.DMA((count - 1,)),
        ],
        compiler_params=pltpu.CompilerParams(collective_id=0, has_side_effects=True),
        name="combine",
    )(partial, mask_table)
    return (zscore, trial_stats)


def solution(mesh):
    in_specs = (P(None, None, ("beam", "tm")), P(), P("beam"))
    out_specs = (P(None, ("beam", "tm")), P(None, "beam"))
    return jax.shard_map(
        per_device, mesh=mesh, in_specs=in_specs, out_specs=out_specs, check_vma=False
    )
```

time: 159 us -> 47.1 us (0.30)
  blocking collectives: 94 us -> 0 us
  Pallas kernels: 0 us -> 38.9 us
  waiting for transfers between devices: 22.7 us -> 0.33 us
  matrix products: 17.3 us -> 0 us
  other arithmetic: 8.09 us -> 0.01 us
  local copies, waits for them, and re-layouts: 7.21 us -> 4.43 us
  starting transfers between devices: 5.18 us -> 2.41 us
  loops' own time: 1.66 us -> 0 us
    psum x2 -> x0, blocking collectives: 64.5 us -> none  [the longest x1 35 us: per_device(): totals = lax.psum(jnp.sum(series, axis=1), 'tm')]
    pallas_call x0 -> x3, Pallas kernels: none -> 38.9 us  [the longest x1 17.7 us: per_device(): pl.pallas_call(functools.partial(combine_kernel, count, frames), out_shap...]
    pmax x1 -> x0, blocking collectives: 29.5 us -> none  [per_device(): peak_value = lax.pmax(jnp.max(series, axis=1), 'tm')]
    ppermute x3 -> x1, waiting for transfers between devices: 22.7 us -> 0.33 us  [per_device(): halo = lax.ppermute(framed[:, frames - (TAPS - 1):], 'tm', steps)]
    dot_general x21 -> x0, matrix products: 17.3 us -> none  [the longest x13 11.5 us: add_group(): jnp.einsum('dsk,skt->dt', selector, stacked, preferred_element_type=jnp.f...]
    while x91 -> x0, local copies, waits for them, and re-layouts: 3.45 us -> none
    ppermute x3 -> x1, starting transfers between devices: 5.18 us -> 2.41 us  [per_device(): halo = lax.ppermute(framed[:, frames - (TAPS - 1):], 'tm', steps)]
    add x14 -> x0, other arithmetic: 2.67 us -> none  [the longest x1 2.62 us: per_device(): weighted + coeffs[tap_index] * extended[:, :, tap_index:tap_index + frame...]
  transfers between devices with their start and end apart: 3 -> 1, of which waited for: 2 -> 1; matrix products, arithmetic and copies ran while one was open for 2% -> 2% of each run, Pallas kernels for 0% -> 0%
where the time goes in v1:
time: 47.1 us; the launch traced here: 46.7 us
  Pallas kernels  38.9 us (83%)
  local copies, waits for them, and re-layouts  4.43 us (9%)
  starting transfers between devices  2.41 us (5%)
  between operations  0.69 us (1%)
    pallas_call x1, Pallas kernels, per_device(): pl.pallas_call(functools.partial(combine_kernel, count, frames), out_shap...  17.7 us
    pallas_call x1, Pallas kernels, per_device(): pl.pallas_call(functools.partial(dedisperse_kernel, frames), out_shape=ja...  15.4 us
    pallas_call x1, Pallas kernels, per_device(): pl.pallas_call(functools.partial(channelize_kernel, frames), out_shape=ja...  5.72 us
    ppermute x1, starting transfers between devices, per_device(): halo = lax.ppermute(framed[:, frames - (TAPS - 1):], 'tm', steps)  2.41 us
    pallas_call x1, local copies, waits for them, and re-layouts, per_device(): pl.pallas_call(functools.partial(combine_kernel, count, frames), out_shap...  1.44 us
    unnamed x7, local copies, waits for them, and re-layouts  1.28 us
    slice x1, local copies, waits for them, and re-layouts, per_device(): halo = lax.ppermute(framed[:, frames - (TAPS - 1):], 'tm', steps)  0.97 us
  transfers between devices with their start and end apart: 1, of which 1 were waited for; matrix products, arithmetic and copies ran while one was open for 2% of the time, Pallas kernels for 0%

profile of v1, /device:TPU:0, one launch (start us, length us, event | category | flops | bytes accessed | tf_op | source)
XLA Modules:
  0.0 46.7 jit_solution(14600601610385091145)
XLA Ops:
  0.6 0.0 copy-start.1
  0.6 1.0 %slice.4 = bf16[2,15,32,128]{3,2,1,0:T(8,128)(2,1)S(1)} slice(bf16[2,32,32,128]{3,2,1,0:T(8,128)(2,1)} %bitcast.6), slice={[0:2], [17:32], [0:32], [0:128]} | slice | bytes 491520 | tf_op jit(solution)/shard_map/slice | solution.py:266
  1.6 2.4 %collective-permute-start = (bf16[2,15,32,128]{3,2,1,0:T(8,128)(2,1)S(1)}, bf16[2,15,32,128]{3,2,1,0:T(8,128)(2,1)S(1)}, u32[]{:S(2)}, u32[]{:S(2)}) collective-permute-start(bf16[2,15,32,128]{3,2,1,0:T(8,128)(2,1)S(1)} %slice.4), channel_id=1, source_target_pairs={{0,1},{1,2},{2,3},{3,4},{4,5},{5,6},{6,7},{7,8},{8,9},{9,10},{10,1... | collective-permute-start | bytes 737288 | tf_op jit(solution)/shard_map/ppermute | solution.py:266
  4.0 0.0 copy-done.1
  4.1 0.1 reshape.15
  4.1 0.7 %copy.11 = f32[128,16]{0,1:T(8,128)} copy(f32[128,16]{1,0:T(8,128)S(1)} %reshape.15) | data formatting | bytes 16384 | tf_op jit(solution)/shard_map/reshape | solution.py:267
  4.8 0.3 collective-permute-done.halo_ref
  5.1 0.0 copy-start
  5.1 0.7 %copy-done = bf16[2,15,32,128]{3,2,1,0:T(8,128)(2,1)} copy-done((bf16[2,15,32,128]{3,2,1,0:T(8,128)(2,1)}, bf16[2,15,32,128]{3,2,1,0:T(8,128)(2,1)S(1)}, u32[]{:S(2)}) %copy-start) | copy-done | bytes 245784
  5.8 5.7 %channelize.1.power_ref = bf16[2048,128]{1,0:T(8,128)(2,1)} custom-call(bf16[2,32,32,128]{3,2,1,0:T(8,128)(2,1)} %bitcast.7, bf16[2,15,32,128]{3,2,1,0:T(8,128)(2,1)} %copy-done, f32[16,32,128]{2,1,0:T(8,128)} %constant.6.clone.taps_ref, f32[2,16,128]{2,1,0:T(8,128)} %constant.7.clone.twid_ref, bf16[2,256,256]{2,1,0:T(8,128)(2,1)} %constant.8.clone.table_ref, ...), custom_call_target="tpu_custom_call" | custom-call | tf_op jit(solution)/shard_map/channelize/pallas_call | solution.py:268
  11.5 15.4 %dedisperse.1.part_ref = f32[64,128]{1,0:T(8,128)} custom-call(s32[64,2048]{1,0:T(8,128)} %delay_ref.1, bf16[2048,128]{1,0:T(8,128)(2,1)} %channelize.1.power_ref), custom_call_target="tpu_custom_call" | custom-call | tf_op jit(solution)/shard_map/dedisperse/pallas_call | solution.py:280
  27.0 17.7 %combine.1 = (f32[64,32]{1,0:T(8,128)}, f32[3,64]{1,0:T(4,128)}) custom-call(f32[64,128]{1,0:T(8,128)} %dedisperse.1.part_ref, f32[16,128]{1,0:T(8,128)} %bitcast.9), custom_call_target="tpu_custom_call" | custom-call | tf_op jit(solution)/shard_map/combine/pallas_call | solution.py:288
  44.7 0.0 copy-start.2
  44.7 1.4 %copy.12 = f32[64,32]{0,1:T(8,128)} copy(f32[64,32]{1,0:T(8,128)} %get-tuple-element.4) | data formatting | bytes 16384 | tf_op jit(solution)/shard_map/combine/pallas_call | solution.py:288
  46.2 0.0 copy-done.2
  46.2 0.6 %copy.14 = f32[3,64]{1,0:T(4,128)} copy(f32[3,64]{1,0:T(4,128)S(1)} %copy-done.2) | data formatting | bytes 1536
  (1 shorter events, 0.0 us)
Async XLA Ops:
  0.6 3.4 %copy-start.1 = (s32[2048]{0:T(1024)S(1)}, s32[2048]{0:T(1024)}, u32[]{:S(2)}) copy-start(s32[2048]{0:T(1024)} %param.8) | copy-start | bytes 24580
  1.6 3.5 %collective-permute-start = (bf16[2,15,32,128]{3,2,1,0:T(8,128)(2,1)S(1)}, bf16[2,15,32,128]{3,2,1,0:T(8,128)(2,1)S(1)}, u32[]{:S(2)}, u32[]{:S(2)}) collective-permute-start(bf16[2,15,32,128]{3,2,1,0:T(8,128)(2,1)S(1)} %slice.4), channel_id=1, source_target_pairs={{0,1},{1,2},{2,3},{3,4},{4,5},{5,6},{6,7},{7,8},{8,9},{9,10},{10,1... | collective-permute-start | bytes 737288 | tf_op jit(solution)/shard_map/ppermute | solution.py:266
  5.1 0.7 %copy-start = (bf16[2,15,32,128]{3,2,1,0:T(8,128)(2,1)}, bf16[2,15,32,128]{3,2,1,0:T(8,128)(2,1)S(1)}, u32[]{:S(2)}) copy-start(bf16[2,15,32,128]{3,2,1,0:T(8,128)(2,1)S(1)} %collective-permute-done.halo_ref) | copy-start | bytes 737284
  44.7 1.5 %copy-start.2 = (f32[3,64]{1,0:T(4,128)S(1)}, f32[3,64]{1,0:T(4,128)}, u32[]{:S(2)}) copy-start(f32[3,64]{1,0:T(4,128)} %get-tuple-element.9) | copy-start | bytes 2308

commit v2 on v1

--- a/solution.py
+++ b/solution.py
@@ -14,8 +14,7 @@
 DSPAN = 3
 LANES = 128
 RADIX = NCHAN // LANES
-BLOCK = 256
-STEP = 4
+STEP = 9
 MESH = pl.DeviceIdType.MESH
 
 
@@ -74,90 +73,161 @@
     return out
 
 
-def channelize_kernel(frames, volt_ref, halo_ref, taps_ref, twid_ref, table_ref, mask_ref, out_ref,
-                      ext, weighted, power):
+def channelize_kernel(count, frames, volt_ref, taps_ref, twid_ref, table_ref, out_ref,
+                      halo, ext, weighted, sections, energy, power, send_sem, recv_sem):
+    me = lax.axis_index("tm")
     past = TAPS - 1
     lines = 2 * RADIX
+    half = frames // 2
+    barrier = pltpu.get_barrier_semaphore()
+
+    def pass_on():
+        return pltpu.make_async_remote_copy(
+            src_ref=volt_ref.at[:, pl.ds(frames - past, past)],
+            dst_ref=halo,
+            send_sem=send_sem,
+            recv_sem=recv_sem,
+            device_id={"tm": me + 1},
+            device_id_type=MESH,
+        )
+
+    @pl.when(me > 0)
+    def _():
+        pl.semaphore_signal(barrier, inc=1, device_id={"tm": me - 1}, device_id_type=MESH)
+
+    @pl.when(me < count - 1)
+    def _():
+        pl.semaphore_wait(barrier, 1)
+        pass_on().start()
+
     for p in range(2):
-        ext[p, 0:past] = halo_ref[p].astype(jnp.float32)
         ext[p, past:past + frames] = volt_ref[p].astype(jnp.float32)
-    for part in range(lines // 8):
-        rows = pl.ds(8 * part, 8)
-        taps = [taps_ref[j, rows, :] for j in range(TAPS)]
-
-        def fir(f, carry):
-            for p in range(2):
-                terms = [taps[j] * ext[p, f + j, rows, :] for j in range(TAPS)]
-                while len(terms) > 1:
-                    terms = [a + b for a, b in zip(terms[0::2], terms[1::2])]
-                start = pl.multiple_of((p * frames + f) * lines, 8) + 8 * part
-                weighted[pl.ds(start, 8), :] = terms[0]
-            return carry
-
-        lax.fori_loop(0, frames, fir, 0, unroll=4)
-
-    rows_all = 2 * frames
-    group = 8
-    high_table = table_ref[0]
-    low_table = table_ref[1]
-    power[...] = jnp.zeros_like(power)
-    sections = [[] for _ in range(RADIX)]
-    for g in range(rows_all // group):
-        items = []
-        for m in range(RADIX):
-            pair = []
-            for c in range(2):
-                start = g * group * lines + 2 * m + c
-                pair.append(weighted[pl.ds(start, group, stride=lines), :])
-            items.append(tuple(pair))
-        for k1, (re, im) in enumerate(butterflies(items)):
-            if k1:
-                c, s = twid_ref[0, k1:k1 + 1, :], twid_ref[1, k1:k1 + 1, :]
-                re, im = re * c - im * s, re * s + im * c
-            sections[k1].append(jnp.concatenate([re, im], axis=1))
-    for k1 in range(RADIX):
-        both = jnp.concatenate(sections[k1], axis=0)
+
+    def fir(begin, end):
+        for part in range(lines // 8):
+            rows = pl.ds(8 * part, 8)
+            taps = [taps_ref[j, rows, :] for j in range(TAPS)]
+
+            def one(f, carry):
+                for p in range(2):
+                    terms = [taps[j] * ext[p, f + j, rows, :] for j in range(TAPS)]
+                    while len(terms) > 1:
+                        terms = [a + b for a, b in zip(terms[0::2], terms[1::2])]
+                    start = pl.multiple_of((p * frames + f) * lines, 8) + 8 * part
+                    weighted[pl.ds(start, 8), :] = terms[0]
+                return carry
+
+            lax.fori_loop(begin, end, one, 0, unroll=4)
+
+    def transform(begin):
+        group = 8
+        rows_half = 2 * half
+        for g in range(rows_half // group):
+            p, f = divmod(g * group, half)
+            first = (p * frames + begin + f) * lines
+            items = []
+            for m in range(RADIX):
+                re = weighted[pl.ds(first + 2 * m, group, stride=lines), :]
+                im = weighted[pl.ds(first + 2 * m + 1, group, stride=lines), :]
+                items.append((re, im))
+            for k1, (re, im) in enumerate(butterflies(items)):
+                if k1:
+                    c, s = twid_ref[0, k1:k1 + 1, :], twid_ref[1, k1:k1 + 1, :]
+                    re, im = re * c - im * s, re * s + im * c
+                place = k1 * rows_half + g * group
+                sections[place:place + group, :LANES] = re
+                sections[place:place + group, LANES:] = im
+        both = sections[...]
         high = both.astype(jnp.bfloat16)
         low = (both - high.astype(jnp.float32)).astype(jnp.bfloat16)
         dot = functools.partial(jnp.dot, preferred_element_type=jnp.float32)
-        spec = dot(high, high_table) + (dot(high, low_table) + dot(low, high_table))
+        spec = dot(high, table_ref[0]) + (dot(high, table_ref[1]) + dot(low, table_ref[0]))
         spec = spec * spec
-        energy = spec[:, :LANES] + spec[:, LANES:]
-        energy = energy[:frames] + energy[frames:]
-        kept = energy.astype(jnp.bfloat16).astype(jnp.float32) * mask_ref[k1:k1 + 1, :]
-        padded = jnp.concatenate([jnp.zeros((LANES - frames, LANES), jnp.float32), kept], axis=0)
+        both_pols = (spec[:, :LANES] + spec[:, LANES:]).reshape(RADIX, 2, half, LANES)
+        energy[:, begin:begin + half, :] = both_pols[:, 0] + both_pols[:, 1]
+
+    fir(half, frames)
+    transform(half)
+
+    @pl.when(me > 0)
+    def _():
+        pass_on().wait_recv()
+        for p in range(2):
+            ext[p, 0:past] = halo[p].astype(jnp.float32)
+
+    @pl.when(me == 0)
+    def _():
+        for p in range(2):
+            ext[p, 0:past] = jnp.zeros((past, lines, LANES), jnp.float32)
+
+    fir(0, half)
+    transform(0)
+    for k1 in range(RADIX):
+        padded = jnp.concatenate([jnp.zeros((LANES - frames, LANES), jnp.float32), energy[k1]], axis=0)
         power[pl.ds(k1, LANES, stride=RADIX), :] = padded.T
     out_ref[...] = power[...].astype(jnp.bfloat16)
 
-
-def dedisperse_kernel(frames, delay_ref, power_ref, out_ref, acc):
+    @pl.when(me < count - 1)
+    def _():
+        pass_on().wait_send()
+
+
+def dedisperse_kernel(frames, delay_ref, mask_ref, power_ref, out_ref, relative, acc):
     trials = delay_ref.shape[0]
     reach = LANES - frames
     bits = max(1, reach.bit_length())
+    blocks = NCHAN // LANES
+    bases = []
+    most = jnp.zeros((trials, 1), jnp.int32)
+    for b in range(blocks):
+        block = delay_ref[:, b * LANES:(b + 1) * LANES]
+        base = block[:, LANES - 1:LANES]
+        bases.append(base)
+        away = block - base
+        most = jnp.maximum(most, away[:, 0:1])
+        away = jnp.where(mask_ref[b:b + 1, :] > 0, away, -1)
+        relative[:, b * LANES:(b + 1) * LANES] = away.astype(jnp.float32).astype(jnp.bfloat16)
+    zeros = jnp.zeros((LANES, LANES), jnp.bfloat16)
+
+    def sweep(first, pair):
+        upper = power_ref[2 * pair * LANES:(2 * pair + 1) * LANES, :]
+        lower = power_ref[(2 * pair + 1) * LANES:(2 * pair + 2) * LANES, :]
+        values = jnp.concatenate(
+            [jnp.concatenate([upper, zeros], axis=1), jnp.concatenate([zeros, lower], axis=1)], axis=0
+        )
+        away = relative[:, 2 * pair * LANES:(2 * pair + 2) * LANES]
+        picks = []
+        for r in range(STEP):
+            target = jnp.asarray(first + r, jnp.float32).astype(jnp.bfloat16)
+            picks.append(jnp.where(away == target, jnp.ones_like(away), jnp.zeros_like(away)))
+        sums = jnp.dot(jnp.concatenate(picks, axis=0), values, preferred_element_type=jnp.float32)
+        out = []
+        for side in range(2):
+            part = sums[:, side * LANES:(side + 1) * LANES]
+            run = part[:trials]
+            for r in range(1, STEP):
+                run = run + pltpu.roll(part[r * trials:(r + 1) * trials], LANES - r, 1)
+            out.append(run)
+        return out
+
+    for pair in range(blocks // 2):
+        for side, run in enumerate(sweep(0, pair)):
+            acc[2 * pair + side] = run
+
+    def more(i, carry):
+        first = i * STEP
+        turn = lax.rem(2 * LANES - first, LANES)
+        for pair in range(blocks // 2):
+            for side, run in enumerate(sweep(first, pair)):
+                acc[2 * pair + side] += pltpu.roll(run, turn, 1)
+        return carry
+
+    lax.fori_loop(1, lax.div(jnp.max(most), STEP) + 1, more, 0)
     total = jnp.zeros((trials, LANES), jnp.float32)
-    for b in range(NCHAN // BLOCK):
-        block = delay_ref[:, b * BLOCK:(b + 1) * BLOCK]
-        base = block[:, BLOCK - 1:BLOCK]
-        relative = block - base
-        most = jnp.max(relative[:, 0:1])
-        values = power_ref[b * BLOCK:(b + 1) * BLOCK, :]
-        acc[...] = jnp.zeros_like(acc)
-
-        def step(i, carry):
-            first = i * STEP
-            shifted = relative - first
-            picks = [jnp.where(shifted == r, 1.0, 0.0).astype(jnp.bfloat16) for r in range(STEP)]
-            sums = jnp.dot(jnp.concatenate(picks, axis=0), values, preferred_element_type=jnp.float32)
-            run = sums[:trials]
-            for r in range(1, STEP):
-                run = run + pltpu.roll(sums[r * trials:(r + 1) * trials], LANES - r, 1)
-            acc[...] += pltpu.roll(run, lax.rem(2 * LANES - first, LANES), 1)
-            return carry
-
-        lax.fori_loop(0, lax.div(most, STEP) + 1, step, 0)
-        moved = acc[...]
+    for b in range(blocks):
+        moved = acc[b]
         for bit in range(bits):
-            chosen = ((base >> bit) & 1) == 1
+            chosen = ((bases[b] >> bit) & 1) == 1
             moved = jnp.where(chosen, pltpu.roll(moved, LANES - (1 << bit), 1), moved)
         total = total + moved
     turned = jnp.concatenate([total, jnp.zeros((LANES - trials, LANES), jnp.float32)], axis=0).T
@@ -192,10 +262,6 @@
         @pl.when(me >= k)
         def _():
             near(k).start()
-
-        @pl.when(me < k)
-        def _():
-            pass
 
     series = part_ref[DSPAN * half:(DSPAN + 1) * half, :]
     for k in range(1, DSPAN + 1):
@@ -242,8 +308,8 @@
     top = jnp.maximum(peak, jnp.max(everyone[:, 2:3, :], axis=0))
     deviation = jnp.sqrt(variance + 1e-05)
     z = (series - average) / deviation
-    z = jnp.concatenate([z, pltpu.roll(z, trials, 1), jnp.zeros((LANES - frames, LANES), jnp.float32)], axis=0).T
-    z_ref[...] = z[:trials, :frames]
+    z_ref[0:half, :] = z[:, :trials]
+    z_ref[half:frames, :] = pltpu.roll(z, trials, 1)[:, :trials]
     stats_ref[...] = jnp.concatenate(
         [average / live, deviation / live, (top - average) / deviation], axis=0
     )[:, :trials]
@@ -262,33 +328,40 @@
     vmem = pl.BlockSpec(memory_space=pltpu.VMEM)
     lines = 2 * RADIX
     framed = voltage.reshape(2, 2, frames * RADIX, LANES).transpose(0, 2, 1, 3).reshape(2, frames, lines, LANES)
-    steps = [(source, source + 1) for source in range(count - 1)]
-    halo = lax.ppermute(framed[:, frames - (TAPS - 1):], "tm", steps)
-    mask_table = chan_mask.astype(jnp.float32).reshape(LANES, RADIX).T
+    mask_table = chan_mask.reshape(RADIX, LANES)
     power = pl.pallas_call(
-        functools.partial(channelize_kernel, frames),
+        functools.partial(channelize_kernel, count, frames),
         out_shape=jax.ShapeDtypeStruct((NCHAN, LANES), jnp.bfloat16),
-        in_specs=[vmem] * 6,
+        in_specs=[vmem] * 4,
         out_specs=vmem,
         scratch_shapes=[
+            pltpu.VMEM((2, TAPS - 1, lines, LANES), jnp.bfloat16),
             pltpu.VMEM((2, frames + TAPS - 1, lines, LANES), jnp.float32),
             pltpu.VMEM((2 * frames * lines, LANES), jnp.float32),
+            pltpu.VMEM((RADIX * frames, 2 * LANES), jnp.float32),
+            pltpu.VMEM((RADIX, frames, LANES), jnp.float32),
             pltpu.VMEM((NCHAN, LANES), jnp.float32),
+            pltpu.SemaphoreType.DMA,
+            pltpu.SemaphoreType.DMA,
         ],
+        compiler_params=pltpu.CompilerParams(collective_id=1, has_side_effects=True),
         name="channelize",
-    )(framed, halo, jnp.asarray(prototype()), jnp.asarray(twiddles()), jnp.asarray(transform_table()), mask_table)
+    )(framed, jnp.asarray(prototype()), jnp.asarray(twiddles()), jnp.asarray(transform_table()))
     partial = pl.pallas_call(
         functools.partial(dedisperse_kernel, frames),
-        out_shape=jax.ShapeDtypeStruct((2 * trials * LANES // LANES // 2, LANES), jnp.float32),
-        in_specs=[vmem] * 2,
+        out_shape=jax.ShapeDtypeStruct((2 * frames, LANES), jnp.float32),
+        in_specs=[vmem] * 3,
         out_specs=vmem,
-        scratch_shapes=[pltpu.VMEM((trials, LANES), jnp.float32)],
+        scratch_shapes=[
+            pltpu.VMEM((trials, NCHAN), jnp.bfloat16),
+            pltpu.VMEM((NCHAN // LANES, trials, LANES), jnp.float32),
+        ],
         name="dedisperse",
-    )(delays, power)
+    )(delays, mask_table, power)
     zscore, trial_stats = pl.pallas_call(
         functools.partial(combine_kernel, count, frames),
         out_shape=(
-            jax.ShapeDtypeStruct((trials, frames), jnp.float32),
+            jax.ShapeDtypeStruct((frames, trials), jnp.float32),
             jax.ShapeDtypeStruct((3, trials), jnp.float32),
         ),
         in_specs=[vmem] * 2,
@@ -305,7 +378,7 @@
         compiler_params=pltpu.CompilerParams(collective_id=0, has_side_effects=True),
         name="combine",
     )(partial, mask_table)
-    return (zscore, trial_stats)
+    return (zscore.T, trial_stats)
 
 
 def solution(mesh):

time: 47.1 us -> 36.2 us (0.77)
  Pallas kernels: 38.9 us -> 33.4 us
  local copies, waits for them, and re-layouts: 4.43 us -> 1.91 us
  starting transfers between devices: 2.41 us -> 0 us
    pallas_call x1, Pallas kernels: 15.4 us -> 10.1 us  [per_device(): pl.pallas_call(functools.partial(dedisperse_kernel, frames), out_shape=ja...]
    ppermute x1 -> x0, starting transfers between devices: 2.41 us -> none  [per_device(): halo = lax.ppermute(framed[:, frames - (TAPS - 1):], 'tm', steps)]
    pallas_call x1 -> x0, local copies, waits for them, and re-layouts: 1.44 us -> none  [per_device(): pl.pallas_call(functools.partial(combine_kernel, count, frames), out_shap...]
    slice x1 -> x0, local copies, waits for them, and re-layouts: 0.97 us -> none  [per_device(): halo = lax.ppermute(framed[:, frames - (TAPS - 1):], 'tm', steps)]
    reshape x2 -> x0, local copies, waits for them, and re-layouts: 0.75 us -> none  [per_device(): mask_table = chan_mask.astype(jnp.float32).reshape(LANES, RADIX).T]
    pallas_call x1, Pallas kernels: 17.7 us -> 17.1 us  [per_device(): pl.pallas_call(functools.partial(combine_kernel, count, frames), out_shap...]
    unnamed x7 -> x4, local copies, waits for them, and re-layouts: 1.28 us -> 1.91 us
    pallas_call x1, Pallas kernels: 5.72 us -> 6.2 us  [per_device(): pl.pallas_call(functools.partial(channelize_kernel, count, frames), out_s...]
  transfers between devices with their start and end apart: 1 -> 0, of which waited for: 1 -> 0; matrix products, arithmetic and copies ran while one was open for 2% -> 0% of each run, Pallas kernels for 0% -> 0%
where the time goes in v2:
time: 36.2 us; the launch traced here: 35.9 us
  Pallas kernels  33.4 us (92%)
  local copies, waits for them, and re-layouts  1.91 us (5%)
  between operations  0.65 us (2%)
    pallas_call x1, Pallas kernels, per_device(): pl.pallas_call(functools.partial(combine_kernel, count, frames), out_shap...  17.1 us
    pallas_call x1, Pallas kernels, per_device(): pl.pallas_call(functools.partial(dedisperse_kernel, frames), out_shape=ja...  10.1 us
    pallas_call x1, Pallas kernels, per_device(): pl.pallas_call(functools.partial(channelize_kernel, count, frames), out_s...  6.2 us
    unnamed x4, local copies, waits for them, and re-layouts  1.91 us

profile of v2, /device:TPU:0, one launch (start us, length us, event | category | flops | bytes accessed | tf_op | source)
XLA Modules:
  0.0 35.9 jit_solution(10045064847537200350)
XLA Ops:
  0.6 6.2 %channelize.1.power_ref = bf16[2048,128]{1,0:T(8,128)(2,1)} custom-call(bf16[2,32,32,128]{3,2,1,0:T(8,128)(2,1)} %bitcast.7, f32[16,32,128]{2,1,0:T(8,128)} %constant.6.clone.taps_ref, f32[2,16,128]{2,1,0:T(8,128)} %constant.7.clone.twid_ref, bf16[2,256,256]{2,1,0:T(8,128)(2,1)} %constant.8.clone.table_ref), custom_call_target="tpu_custom_call" | custom-call | tf_op jit(solution)/shard_map/channelize/pallas_call | solution.py:332
  6.8 10.1 %dedisperse.1.part_ref = f32[64,128]{1,0:T(8,128)} custom-call(s32[64,2048]{1,0:T(8,128)} %delay_ref.1, s32[16,128]{1,0:T(8,128)} %bitcast.8, bf16[2048,128]{1,0:T(8,128)(2,1)} %channelize.1.power_ref), custom_call_target="tpu_custom_call" | custom-call | tf_op jit(solution)/shard_map/dedisperse/pallas_call | solution.py:350
  16.9 17.1 %combine.1 = (f32[32,64]{1,0:T(8,128)}, f32[3,64]{1,0:T(4,128)}) custom-call(f32[64,128]{1,0:T(8,128)} %dedisperse.1.part_ref, s32[16,128]{1,0:T(8,128)} %bitcast.9), custom_call_target="tpu_custom_call" | custom-call | tf_op jit(solution)/shard_map/combine/pallas_call | solution.py:361
  34.0 0.0 copy-start
  34.0 1.3 %copy.11 = f32[64,32]{0,1:T(8,128)} copy(f32[64,32]{0,1:T(8,128)} %bitcast.10) | data formatting | bytes 16384
  35.4 0.0 copy-done
  35.4 0.6 %copy.12 = f32[3,64]{1,0:T(4,128)} copy(f32[3,64]{1,0:T(4,128)S(1)} %copy-done) | data formatting | bytes 1536
Async XLA Ops:
  34.0 1.3 %copy-start = (f32[3,64]{1,0:T(4,128)S(1)}, f32[3,64]{1,0:T(4,128)}, u32[]{:S(2)}) copy-start(f32[3,64]{1,0:T(4,128)} %get-tuple-element.9) | copy-start | bytes 2308

commit v3 on v2

--- a/solution.py
+++ b/solution.py
@@ -15,6 +15,7 @@
 LANES = 128
 RADIX = NCHAN // LANES
 STEP = 9
+GRANT = 16 * 1024 * 1024
 MESH = pl.DeviceIdType.MESH
 
 
@@ -73,20 +74,24 @@
     return out
 
 
-def channelize_kernel(count, frames, volt_ref, taps_ref, twid_ref, table_ref, out_ref,
-                      halo, ext, weighted, sections, energy, power, send_sem, recv_sem):
+def channelize_kernel(count, frames, volt_ref, taps_ref, twid_ref, table_ref, delay_ref, mask_ref, out_ref,
+                      relative_ref, meta_ref, halo, ext, weighted, sections, energy, power, send_sem, recv_sem):
     me = lax.axis_index("tm")
     past = TAPS - 1
     lines = 2 * RADIX
     half = frames // 2
+    quarter = frames // 4
+    cut = min(quarter, past - 1)
+    spans = ((cut, past - cut), (0, cut))
     barrier = pltpu.get_barrier_semaphore()
 
-    def pass_on():
+    def pass_on(i):
+        begin, size = spans[i]
         return pltpu.make_async_remote_copy(
-            src_ref=volt_ref.at[:, pl.ds(frames - past, past)],
-            dst_ref=halo,
-            send_sem=send_sem,
-            recv_sem=recv_sem,
+            src_ref=volt_ref.at[:, pl.ds(frames - past + begin, size)],
+            dst_ref=halo.at[:, pl.ds(begin, size)],
+            send_sem=send_sem.at[i],
+            recv_sem=recv_sem.at[i],
             device_id={"tm": me + 1},
             device_id_type=MESH,
         )
@@ -98,7 +103,8 @@
     @pl.when(me < count - 1)
     def _():
         pl.semaphore_wait(barrier, 1)
-        pass_on().start()
+        pass_on(0).start()
+        pass_on(1).start()
 
     for p in range(2):
         ext[p, past:past + frames] = volt_ref[p].astype(jnp.float32)
@@ -119,11 +125,11 @@
 
             lax.fori_loop(begin, end, one, 0, unroll=4)
 
-    def transform(begin):
+    def transform(begin, size):
         group = 8
-        rows_half = 2 * half
+        rows_half = 2 * size
         for g in range(rows_half // group):
-            p, f = divmod(g * group, half)
+            p, f = divmod(g * group, size)
             first = (p * frames + begin + f) * lines
             items = []
             for m in range(RADIX):
@@ -137,31 +143,49 @@
                 place = k1 * rows_half + g * group
                 sections[place:place + group, :LANES] = re
                 sections[place:place + group, LANES:] = im
-        both = sections[...]
+        both = sections[0:RADIX * rows_half, :]
         high = both.astype(jnp.bfloat16)
         low = (both - high.astype(jnp.float32)).astype(jnp.bfloat16)
         dot = functools.partial(jnp.dot, preferred_element_type=jnp.float32)
         spec = dot(high, table_ref[0]) + (dot(high, table_ref[1]) + dot(low, table_ref[0]))
         spec = spec * spec
-        both_pols = (spec[:, :LANES] + spec[:, LANES:]).reshape(RADIX, 2, half, LANES)
-        energy[:, begin:begin + half, :] = both_pols[:, 0] + both_pols[:, 1]
+        both_pols = (spec[:, :LANES] + spec[:, LANES:]).reshape(RADIX, 2, size, LANES)
+        energy[:, begin:begin + size, :] = both_pols[:, 0] + both_pols[:, 1]
 
     fir(half, frames)
-    transform(half)
-
-    @pl.when(me > 0)
-    def _():
-        pass_on().wait_recv()
-        for p in range(2):
-            ext[p, 0:past] = halo[p].astype(jnp.float32)
-
-    @pl.when(me == 0)
-    def _():
-        for p in range(2):
-            ext[p, 0:past] = jnp.zeros((past, lines, LANES), jnp.float32)
-
-    fir(0, half)
-    transform(0)
+    transform(half, frames - half)
+    trials = delay_ref.shape[0]
+    blocks = NCHAN // LANES
+    lane = lax.broadcasted_iota(jnp.int32, (trials, LANES), 1)
+    meta = jnp.zeros((trials, LANES), jnp.int32)
+    most = jnp.zeros((trials, 1), jnp.int32)
+    for b in range(blocks):
+        block = delay_ref[:, b * LANES:(b + 1) * LANES]
+        base = block[:, LANES - 1:LANES]
+        away = block - base
+        most = jnp.maximum(most, away[:, 0:1])
+        meta = jnp.where(lane == b, base, meta)
+        away = jnp.where(mask_ref[b:b + 1, :] > 0, away, -1)
+        relative_ref[:, b * LANES:(b + 1) * LANES] = away.astype(jnp.float32).astype(jnp.bfloat16)
+    meta_ref[...] = jnp.where(lane == blocks, most, meta)
+
+    for i, (begin, end) in enumerate(((quarter, half), (0, quarter))):
+        first, size = spans[i]
+
+        @pl.when(me > 0)
+        def _():
+            pass_on(i).wait_recv()
+            for p in range(2):
+                ext[p, first:first + size] = halo[p, first:first + size].astype(jnp.float32)
+
+        @pl.when(me == 0)
+        def _():
+            for p in range(2):
+                ext[p, first:first + size] = jnp.zeros((size, lines, LANES), jnp.float32)
+
+        fir(begin, end)
+        transform(begin, end - begin)
+
     for k1 in range(RADIX):
         padded = jnp.concatenate([jnp.zeros((LANES - frames, LANES), jnp.float32), energy[k1]], axis=0)
         power[pl.ds(k1, LANES, stride=RADIX), :] = padded.T
@@ -169,24 +193,14 @@
 
     @pl.when(me < count - 1)
     def _():
-        pass_on().wait_send()
-
-
-def dedisperse_kernel(frames, delay_ref, mask_ref, power_ref, out_ref, relative, acc):
-    trials = delay_ref.shape[0]
-    reach = LANES - frames
-    bits = max(1, reach.bit_length())
+        pass_on(0).wait_send()
+        pass_on(1).wait_send()
+
+
+def dedisperse_kernel(frames, relative, meta_ref, power_ref, out_ref, acc):
+    trials = relative.shape[0]
     blocks = NCHAN // LANES
-    bases = []
-    most = jnp.zeros((trials, 1), jnp.int32)
-    for b in range(blocks):
-        block = delay_ref[:, b * LANES:(b + 1) * LANES]
-        base = block[:, LANES - 1:LANES]
-        bases.append(base)
-        away = block - base
-        most = jnp.maximum(most, away[:, 0:1])
-        away = jnp.where(mask_ref[b:b + 1, :] > 0, away, -1)
-        relative[:, b * LANES:(b + 1) * LANES] = away.astype(jnp.float32).astype(jnp.bfloat16)
+    most = meta_ref[:, blocks:blocks + 1]
     zeros = jnp.zeros((LANES, LANES), jnp.bfloat16)
 
     def sweep(first, pair):
@@ -223,13 +237,11 @@
         return carry
 
     lax.fori_loop(1, lax.div(jnp.max(most), STEP) + 1, more, 0)
+    lane = lax.broadcasted_iota(jnp.int32, (trials, LANES), 1)
     total = jnp.zeros((trials, LANES), jnp.float32)
     for b in range(blocks):
-        moved = acc[b]
-        for bit in range(bits):
-            chosen = ((bases[b] >> bit) & 1) == 1
-            moved = jnp.where(chosen, pltpu.roll(moved, LANES - (1 << bit), 1), moved)
-        total = total + moved
+        place = (lane + meta_ref[:, b:b + 1]) & (LANES - 1)
+        total = total + jnp.take_along_axis(acc[b], place, axis=1, mode="promise_in_bounds")
     turned = jnp.concatenate([total, jnp.zeros((LANES - trials, LANES), jnp.float32)], axis=0).T
     half = frames // 2
     for s in range(LANES // frames):
@@ -329,11 +341,15 @@
     lines = 2 * RADIX
     framed = voltage.reshape(2, 2, frames * RADIX, LANES).transpose(0, 2, 1, 3).reshape(2, frames, lines, LANES)
     mask_table = chan_mask.reshape(RADIX, LANES)
-    power = pl.pallas_call(
+    power, relative, meta = pl.pallas_call(
         functools.partial(channelize_kernel, count, frames),
-        out_shape=jax.ShapeDtypeStruct((NCHAN, LANES), jnp.bfloat16),
-        in_specs=[vmem] * 4,
-        out_specs=vmem,
+        out_shape=(
+            jax.ShapeDtypeStruct((NCHAN, LANES), jnp.bfloat16),
+            jax.ShapeDtypeStruct((trials, NCHAN), jnp.bfloat16),
+            jax.ShapeDtypeStruct((trials, LANES), jnp.int32),
+        ),
+        in_specs=[vmem] * 6,
+        out_specs=(vmem,) * 3,
         scratch_shapes=[
             pltpu.VMEM((2, TAPS - 1, lines, LANES), jnp.bfloat16),
             pltpu.VMEM((2, frames + TAPS - 1, lines, LANES), jnp.float32),
@@ -341,23 +357,23 @@
             pltpu.VMEM((RADIX * frames, 2 * LANES), jnp.float32),
             pltpu.VMEM((RADIX, frames, LANES), jnp.float32),
             pltpu.VMEM((NCHAN, LANES), jnp.float32),
-            pltpu.SemaphoreType.DMA,
-            pltpu.SemaphoreType.DMA,
+            pltpu.SemaphoreType.DMA((2,)),
+            pltpu.SemaphoreType.DMA((2,)),
         ],
-        compiler_params=pltpu.CompilerParams(collective_id=1, has_side_effects=True),
+        compiler_params=pltpu.CompilerParams(collective_id=1, vmem_limit_bytes=GRANT, has_side_effects=True),
         name="channelize",
-    )(framed, jnp.asarray(prototype()), jnp.asarray(twiddles()), jnp.asarray(transform_table()))
+    )(framed, jnp.asarray(prototype()), jnp.asarray(twiddles()), jnp.asarray(transform_table()), delays, mask_table)
     partial = pl.pallas_call(
         functools.partial(dedisperse_kernel, frames),
         out_shape=jax.ShapeDtypeStruct((2 * frames, LANES), jnp.float32),
         in_specs=[vmem] * 3,
         out_specs=vmem,
         scratch_shapes=[
-            pltpu.VMEM((trials, NCHAN), jnp.bfloat16),
             pltpu.VMEM((NCHAN // LANES, trials, LANES), jnp.float32),
         ],
+        compiler_params=pltpu.CompilerParams(vmem_limit_bytes=GRANT),
         name="dedisperse",
-    )(delays, mask_table, power)
+    )(relative, meta, power)
     zscore, trial_stats = pl.pallas_call(
         functools.partial(combine_kernel, count, frames),
         out_shape=(
@@ -375,7 +391,7 @@
             pltpu.SemaphoreType.DMA((count - 1,)),
             pltpu.SemaphoreType.DMA((count - 1,)),
         ],
-        compiler_params=pltpu.CompilerParams(collective_id=0, has_side_effects=True),
+        compiler_params=pltpu.CompilerParams(collective_id=0, vmem_limit_bytes=GRANT, has_side_effects=True),
         name="combine",
     )(partial, mask_table)
     return (zscore.T, trial_stats)

time: 36.2 us -> 29.6 us (0.82)
  Pallas kernels: 33.4 us -> 22 us
  local copies, waits for them, and re-layouts: 1.91 us -> 6.57 us
    pallas_call x1, Pallas kernels: 10.1 us -> 2.76 us  [per_device(): pl.pallas_call(functools.partial(dedisperse_kernel, frames), out_shape=ja...]
    unnamed x4 -> x14, local copies, waits for them, and re-layouts: 1.91 us -> 6.57 us
    pallas_call x1, Pallas kernels: 17.1 us -> 14.9 us  [per_device(): pl.pallas_call(functools.partial(combine_kernel, count, frames), out_shap...]
    pallas_call x1, Pallas kernels: 6.2 us -> 4.39 us  [per_device(): pl.pallas_call(functools.partial(channelize_kernel, count, frames), out_s...]
where the time goes in v3:
time: 29.6 us; the launch traced here: 29.3 us
  Pallas kernels  22 us (74%)
  local copies, waits for them, and re-layouts  6.57 us (22%)
  between operations  0.67 us (2%)
    pallas_call x1, Pallas kernels, per_device(): pl.pallas_call(functools.partial(combine_kernel, count, frames), out_shap...  14.9 us
    unnamed x14, local copies, waits for them, and re-layouts  6.57 us
    pallas_call x1, Pallas kernels, per_device(): pl.pallas_call(functools.partial(channelize_kernel, count, frames), out_s...  4.39 us
    pallas_call x1, Pallas kernels, per_device(): pl.pallas_call(functools.partial(dedisperse_kernel, frames), out_shape=ja...  2.76 us

profile of v3, /device:TPU:0, one launch (start us, length us, event | category | flops | bytes accessed | tf_op | source)
XLA Modules:
  0.0 29.3 jit_solution(3998883056904957251)
XLA Ops:
  0.6 0.0 copy-start
  0.6 1.0 %copy-done = bf16[2,2,65536]{2,1,0:T(2,128)(2,1)S(1)} copy-done((bf16[2,2,65536]{2,1,0:T(2,128)(2,1)S(1)}, bf16[2,2,65536]{2,1,0:T(2,128)(2,1)}, u32[]{:S(2)}) %copy-start) | copy-done | bytes 524312
  1.7 0.0 copy-start.1
  1.7 1.0 %copy-done.1 = s32[64,2048]{1,0:T(8,128)S(1)} copy-done((s32[64,2048]{1,0:T(8,128)S(1)}, s32[64,2048]{1,0:T(8,128)}, u32[]{:S(2)}) %copy-start.1) | copy-done | bytes 524312
  2.7 0.0 copy-start.2
  2.7 0.9 %copy-done.2 = bf16[2,256,256]{2,1,0:T(8,128)(2,1)S(1)} copy-done((bf16[2,256,256]{2,1,0:T(8,128)(2,1)S(1)}, bf16[2,256,256]{2,1,0:T(8,128)(2,1)}, u32[]{:S(2)}) %copy-start.2) | copy-done | bytes 262168
  3.7 0.0 copy-start.3
  3.7 0.9 %copy-done.3 = f32[16,32,128]{2,1,0:T(8,128)S(1)} copy-done((f32[16,32,128]{2,1,0:T(8,128)S(1)}, f32[16,32,128]{2,1,0:T(8,128)}, u32[]{:S(2)}) %copy-start.3) | copy-done | bytes 262168
  4.6 0.0 copy-start.4
  4.6 0.7 %copy-done.4 = s32[2048]{0:T(1024)S(1)} copy-done((s32[2048]{0:T(1024)S(1)}, s32[2048]{0:T(1024)}, u32[]{:S(2)}) %copy-start.4) | copy-done | bytes 8216
  5.3 0.0 copy-start.5
  5.3 0.7 %copy-done.5 = f32[2,16,128]{2,1,0:T(8,128)S(1)} copy-done((f32[2,16,128]{2,1,0:T(8,128)S(1)}, f32[2,16,128]{2,1,0:T(8,128)}, u32[]{:S(2)}) %copy-start.5) | copy-done | bytes 16408
  6.0 4.4 %channelize.1 = (bf16[2048,128]{1,0:T(8,128)(2,1)S(1)}, bf16[64,2048]{1,0:T(8,128)(2,1)S(1)}, s32[64,128]{1,0:T(8,128)S(1)}) custom-call(bf16[2,32,32,128]{3,2,1,0:T(8,128)(2,1)S(1)} %bitcast.7, f32[16,32,128]{2,1,0:T(8,128)S(1)} %copy-done.3, f32[2,16,128]{2,1,0:T(8,128)S(1)} %copy-done.5, bf16[2,256,256]{2,1,0:T(8,128)(2,1)S(1)} %copy-done.2, ...), custom_call_target="tpu_custom_call" | custom-call | tf_op jit(solution)/shard_map/channelize/pallas_call | solution.py:344
  10.4 2.8 %dedisperse.1.part_ref = f32[64,128]{1,0:T(8,128)S(1)} custom-call(bf16[64,2048]{1,0:T(8,128)(2,1)S(1)} %get-tuple-element.7.relative, s32[64,128]{1,0:T(8,128)S(1)} %get-tuple-element.8.meta_ref, bf16[2048,128]{1,0:T(8,128)(2,1)S(1)} %get-tuple-element.9.power_ref), custom_call_target="tpu_custom_call" | custom-call | tf_op jit(solution)/shard_map/dedisperse/pallas_call | solution.py:366
  13.2 14.9 %combine.1 = (f32[32,64]{1,0:T(8,128)S(1)}, f32[3,64]{1,0:T(4,128)S(1)}) custom-call(f32[64,128]{1,0:T(8,128)S(1)} %dedisperse.1.part_ref, s32[16,128]{1,0:T(8,128)S(1)} %bitcast.9), custom_call_target="tpu_custom_call" | custom-call | tf_op jit(solution)/shard_map/combine/pallas_call | solution.py:377
  28.1 0.6 %copy.11 = f32[64,32]{0,1:T(8,128)} copy(f32[64,32]{0,1:T(8,128)S(1)} %bitcast.10) | data formatting | bytes 16384
  28.7 0.6 %copy.12 = f32[3,64]{1,0:T(4,128)} copy(f32[3,64]{1,0:T(4,128)S(1)} %get-tuple-element.15) | data formatting | bytes 1536
Async XLA Ops:
  0.6 1.0 %copy-start = (bf16[2,2,65536]{2,1,0:T(2,128)(2,1)S(1)}, bf16[2,2,65536]{2,1,0:T(2,128)(2,1)}, u32[]{:S(2)}) copy-start(bf16[2,2,65536]{2,1,0:T(2,128)(2,1)} %param.6) | copy-start | bytes 1572868
  1.7 1.0 %copy-start.1 = (s32[64,2048]{1,0:T(8,128)S(1)}, s32[64,2048]{1,0:T(8,128)}, u32[]{:S(2)}) copy-start(s32[64,2048]{1,0:T(8,128)} %delay_ref.1) | copy-start | bytes 1572868
  2.7 0.9 %copy-start.2 = (bf16[2,256,256]{2,1,0:T(8,128)(2,1)S(1)}, bf16[2,256,256]{2,1,0:T(8,128)(2,1)}, u32[]{:S(2)}) copy-start(bf16[2,256,256]{2,1,0:T(8,128)(2,1)} %constant.8.clone.table_ref) | copy-start | bytes 786436
  3.7 0.9 %copy-start.3 = (f32[16,32,128]{2,1,0:T(8,128)S(1)}, f32[16,32,128]{2,1,0:T(8,128)}, u32[]{:S(2)}) copy-start(f32[16,32,128]{2,1,0:T(8,128)} %constant.6.clone.taps_ref) | copy-start | bytes 786436
  4.6 0.7 %copy-start.4 = (s32[2048]{0:T(1024)S(1)}, s32[2048]{0:T(1024)}, u32[]{:S(2)}) copy-start(s32[2048]{0:T(1024)} %param.8) | copy-start | bytes 24580
  5.3 0.7 %copy-start.5 = (f32[2,16,128]{2,1,0:T(8,128)S(1)}, f32[2,16,128]{2,1,0:T(8,128)}, u32[]{:S(2)}) copy-start(f32[2,16,128]{2,1,0:T(8,128)} %constant.7.clone.twid_ref) | copy-start | bytes 49156
